TPU v7x, 32 devices: a whole 2x2x4 slice. The times are simulated.
32 devices in a mesh: ens: 4 (over y, x), slab: 8 (over z, core).
Axes of the slice: x: 2, y: 2, z: 4, core: 2. Of those that a mesh axis runs over, the one named last changes fastest.
Arguments:
- density0: float32 [192, 1024], P('slab'), may hold values from 0.5 to 1.5
- relax_rate: float32 [192, 1024], P('slab'), may hold values from 0.6 to 1.8
- perturbation: int32 [4, 192, 1024], P('ens', 'slab'), may hold values from -3 to 3
Outputs:
- lifted: float32 [4, 9, 192, 1024], P('ens', None, 'slab')
- projected: float32 [192, 1024], P('slab')
All inputs are finite; a program needn't handle non-finite values.
Results may differ from a plain program's by a relative error of at most 0.0002.
Values sent between devices are 32-bit elements; how exact they have to be, the bound alone decides.
A program may use at most 64 MiB of HBM per device.

v0:
```python
import functools

import jax
import jax.numpy as jnp
from jax import lax
from jax.experimental import pallas as pl
from jax.experimental.pallas import tpu as pltpu
from jax.sharding import PartitionSpec as P

MICRO_SPELLS = 3
STEPS = 8
TOTAL = MICRO_SPELLS * STEPS
LANES = 128
CHUNK = 4
BIG = 12
FIRST = 12
FRONT = 8

row_moves = (0, 0, 1, 0, -1, 1, 1, -1, -1)
col_moves = (0, 1, 0, -1, 0, 1, -1, -1, 1)
lattice_weights = (4.0 / 9.0,) + (1.0 / 9.0,) * 4 + (1.0 / 36.0,) * 4
shift_amp = 0.08
step_cap = 0.25
MESH = pl.DeviceIdType.MESH


def roll_columns(x, move):
    if move == 0:
        return x
    subs = x.shape[1]
    lane = lax.broadcasted_iota(jnp.int32, x.shape, 2)
    if move == 1:
        within = pltpu.roll(x, 1, 2)
        across = pltpu.roll(within, 1, 1)
        return jnp.where(lane == 0, across, within)
    within = pltpu.roll(x, LANES - 1, 2)
    across = pltpu.roll(within, subs - 1, 1)
    return jnp.where(lane == LANES - 1, across, within)


def collide(f, keep, third, ninth):
    s13, d13 = f[1] + f[3], f[1] - f[3]
    s24, d24 = f[2] + f[4], f[2] - f[4]
    s57, d57 = f[5] + f[7], f[5] - f[7]
    s68, d68 = f[6] + f[8], f[6] - f[8]
    density = (f[0] + (s13 + s24)) + (s57 + s68)
    mom_row = d24 + (d57 + d68)
    mom_col = d13 + (d57 - d68)
    inverse = 1.5 / density
    vel_row = mom_row * inverse
    vel_col = mom_col * inverse
    third_row = third * mom_row
    third_col = third * mom_col
    half_rr = third_row * vel_row
    half_cc = third_col * vel_col
    quarter_rc = (third_row * vel_col) * 0.5
    squares = half_rr + half_cc
    base = ninth * density - squares * (1.0 / 3.0)
    even_col = base + half_cc
    even_row = base + half_rr
    corner = 0.25 * (base + squares)
    even_57 = corner + quarter_rc
    even_68 = corner - quarter_rc
    odd_57 = 0.25 * (third_row + third_col)
    odd_68 = 0.25 * (third_row - third_col)
    k = [keep * value for value in f]
    return (
        k[0] + 4.0 * base,
        k[1] + (even_col + third_col),
        k[2] + (even_row + third_row),
        k[3] + (even_col - third_col),
        k[4] + (even_row - third_row),
        k[5] + (even_57 + odd_57),
        k[6] + (even_68 + odd_68),
        k[7] + (even_57 - odd_57),
        k[8] + (even_68 - odd_68),
    )


def kernel(
    ens,
    slabs,
    density_in,
    relax_in,
    pert_in,
    finals,
    scale_out,
    projected_out,
    start,
    relax,
    coef,
    buf,
    gathered,
    squares,
    halo_send,
    halo_recv,
    ens_send,
    ens_recv,
    sq_send,
    sq_recv,
):
    height, width = density_in.shape
    subs = width // LANES
    rows = height + 2 * TOTAL
    me_e = lax.axis_index("ens")
    me_s = lax.axis_index("slab")

    barrier = pltpu.get_barrier_semaphore()
    for k in range(1, ens):
        pl.semaphore_signal(
            barrier, inc=1, device_id={"ens": lax.rem(me_e + k, ens)}, device_id_type=MESH
        )
    for k in range(1, slabs):
        pl.semaphore_signal(
            barrier, inc=1, device_id={"slab": lax.rem(me_s + k, slabs)}, device_id_type=MESH
        )

    own = pl.ds(TOTAL, height)
    for s in range(subs):
        relax[own, s, :] = relax_in[:, s * LANES : (s + 1) * LANES]
    for s in range(subs):
        cols = slice(s * LANES, (s + 1) * LANES)
        start[own, s, :] = density_in[:, cols] + shift_amp * pert_in[0, :, cols].astype(jnp.float32)

    def first_rows(low, high):
        def body(c, carry):
            at = pl.ds(low + c * FIRST, FIRST)
            fresh = start[at]
            rate = relax[at]
            rates = (1.0 - rate, rate * (1.0 / 3.0), rate * (1.0 / 9.0))
            for n in range(3):
                coef[n, at] = rates[n]
            out = collide([weight * fresh for weight in lattice_weights], *rates)
            for i in range(9):
                buf[1, i, pl.ds(FRONT + low + c * FIRST, FIRST)] = roll_columns(out[i], col_moves[i])
            return carry

        lax.fori_loop(0, (high - low) // FIRST, body, 0)

    first_rows(TOTAL, TOTAL + height)
    pl.semaphore_wait(barrier, ens + slabs - 2)
    right = lax.rem(me_s + 1, slabs)
    left = lax.rem(me_s + slabs - 1, slabs)
    halos = []
    for n, field in enumerate((relax, start)):
        for side, (target, source, dest) in enumerate(
            ((right, height, 0), (left, TOTAL, TOTAL + height))
        ):
            halos.append(
                pltpu.make_async_remote_copy(
                    src_ref=field.at[pl.ds(source, TOTAL)],
                    dst_ref=field.at[pl.ds(dest, TOTAL)],
                    send_sem=halo_send.at[n, side],
                    recv_sem=halo_recv.at[n, side],
                    device_id={"slab": target},
                    device_id_type=MESH,
                )
            )
    for copy in halos:
        copy.start()

    def step(k, carry):
        source, dest = lax.rem(k + 1, 2), lax.rem(k, 2)

        def sweep(low, chunks, size):
            def body(c, inner):
                at = FRONT + low + c * size
                f = [buf[source, i, pl.ds(at - row_moves[i], size)] for i in range(9)]
                out = collide(f, *(coef[n, pl.ds(at - FRONT, size)] for n in range(3)))
                for i in range(9):
                    buf[dest, i, pl.ds(at, size)] = roll_columns(out[i], col_moves[i])
                return inner

            lax.fori_loop(0, chunks, body, 0)

        count = rows - 2 * k + 2
        whole = (count + CHUNK // 2) // BIG
        sweep(k - 1, whole, BIG)
        rest = jnp.maximum(count - whole * BIG, 0)
        sweep(k - 1 + whole * BIG, (rest + CHUNK - 1) // CHUNK, CHUNK)
        return carry

    def spell_density(spell, parity):
        def body(c, inner):
            at = FRONT + TOTAL + c * CHUNK
            total = buf[parity, 0, pl.ds(at, CHUNK)]
            for i in range(1, 9):
                total = total + buf[parity, i, pl.ds(at - row_moves[i], CHUNK)]
            gathered[spell, me_e, pl.ds(c * CHUNK, CHUNK)] = total
            return inner

        lax.fori_loop(0, height // CHUNK, body, 0)
        copies = []
        for k in range(1, ens):
            copies.append(
                pltpu.make_async_remote_copy(
                    src_ref=gathered.at[spell, me_e],
                    dst_ref=gathered.at[spell, me_e],
                    send_sem=ens_send.at[spell, k - 1],
                    recv_sem=ens_recv.at[spell, k - 1],
                    device_id={"ens": lax.rem(me_e + k, ens)},
                    device_id_type=MESH,
                )
            )
        for copy in copies:
            copy.start()
        return copies

    for copy in halos:
        copy.wait_recv()
    first_rows(0, TOTAL)
    first_rows(TOTAL + height, rows)

    sent = []
    for spell in range(MICRO_SPELLS):
        lax.fori_loop(max(2, spell * STEPS + 1), (spell + 1) * STEPS + 1, step, 0)
        sent.append(spell_density(spell, ((spell + 1) * STEPS) % 2))

    parity = TOTAL % 2
    for s in range(subs):
        cols = slice(s * LANES, (s + 1) * LANES)
        for i in range(9):
            finals[i, :, cols] = buf[parity, i, pl.ds(FRONT + TOTAL - row_moves[i], height), s, :]

    for copies in sent:
        for copy in copies:
            copy.wait_recv()

    def mean(spell, at):
        total = gathered[spell, 0, at]
        for member in range(1, ens):
            total = total + gathered[spell, member, at]
        return total * (1.0 / ens)

    def fit(c, acc):
        at = pl.ds(c * CHUNK, CHUNK)
        first, middle, last = (mean(spell, at) for spell in range(MICRO_SPELLS))
        change = last - first
        start[at] = change
        relax[at] = (first + middle + last) * (1.0 / 3.0) + 0.5 * change
        return acc + jnp.sum(change * change, axis=0)

    acc = lax.fori_loop(0, height // CHUNK, fit, jnp.zeros((subs, LANES), jnp.float32))
    squares[me_s] = acc
    copies = []
    for k in range(1, slabs):
        copies.append(
            pltpu.make_async_remote_copy(
                src_ref=squares.at[me_s],
                dst_ref=squares.at[me_s],
                send_sem=sq_send.at[k - 1],
                recv_sem=sq_recv.at[k - 1],
                device_id={"slab": lax.rem(me_s + k, slabs)},
                device_id_type=MESH,
            )
        )
    for copy in copies:
        copy.start()
    for copy in copies:
        copy.wait_recv()
    total = jnp.sum(jnp.sum(squares[...], axis=0), axis=(0, 1), keepdims=True)
    mean_square = total * (1.0 / (height * width * slabs))
    gain = (step_cap / jnp.sqrt(mean_square + 1e-06))[None]
    field = pl.ds(0, height)
    projected = relax[field] + gain * start[field]
    start[field] = projected
    relax[field] = projected / gathered[MICRO_SPELLS - 1, me_e]
    for s in range(subs):
        cols = slice(s * LANES, (s + 1) * LANES)
        projected_out[:, cols] = start[field, s, :]
        scale_out[:, cols] = relax[field, s, :]

    for group in [halos, copies] + sent:
        for copy in group:
            copy.wait_send()


def on_device(density0, relax_rate, perturbation):
    height, width = density0.shape
    ens, slabs = lax.axis_size("ens"), lax.axis_size("slab")
    assert perturbation.shape[0] == 1 and height >= TOTAL and width % LANES == 0
    assert height % CHUNK == 0 and CHUNK <= FRONT
    assert height % FIRST == 0 and TOTAL % FIRST == 0
    subs = width // LANES
    rows = height + 2 * TOTAL + max(CHUNK, FIRST)
    f32 = jnp.float32
    field = jax.ShapeDtypeStruct((height, width), f32)
    vmem = pl.BlockSpec(memory_space=pltpu.VMEM)
    dma = pltpu.SemaphoreType.DMA
    finals, scale, projected = pl.pallas_call(
        functools.partial(kernel, ens, slabs),
        out_shape=(
            jax.ShapeDtypeStruct((9, height, width), f32),
            field,
            field,
        ),
        in_specs=[vmem] * 3,
        out_specs=[vmem] * 3,
        scratch_shapes=[
            pltpu.VMEM((rows, subs, LANES), f32),
            pltpu.VMEM((rows, subs, LANES), f32),
            pltpu.VMEM((3, rows, subs, LANES), f32),
            pltpu.VMEM((2, 9, rows + FRONT, subs, LANES), f32),
            pltpu.VMEM((MICRO_SPELLS, ens, height, subs, LANES), f32),
            pltpu.VMEM((slabs, subs, LANES), f32),
            dma((2, 2)),
            dma((2, 2)),
            dma((MICRO_SPELLS, ens - 1)),
            dma((MICRO_SPELLS, ens - 1)),
            dma((slabs - 1,)),
            dma((slabs - 1,)),
        ],
        compiler_params=pltpu.CompilerParams(
            collective_id=0, has_side_effects=True, vmem_limit_bytes=24 << 20
        ),
    )(density0, relax_rate, perturbation)
    lifted = finals * scale[None]
    return (lifted[None], projected)


def solution(mesh):
    in_specs = (P("slab", None), P("slab", None), P("ens", "slab", None))
    out_specs = (P("ens", None, "slab", None), P("slab", None))
    return jax.shard_map(
        on_device, mesh=mesh, in_specs=in_specs, out_specs=out_specs, check_vma=False
    )
```

profile of v0, /device:TPU:0, one launch (start us, length us, event | category | flops | bytes accessed | tf_op | source)
XLA Modules:
  0.0 50.5 jit_solution(17582079595909917068)
XLA Ops:
  0.6 0.0 copy-start
  0.6 0.9 %copy-done = f32[24,1024]{1,0:T(8,128)S(1)} copy-done((f32[24,1024]{1,0:T(8,128)S(1)}, f32[24,1024]{1,0:T(8,128)}, u32[]{:S(2)}) %copy-start) | copy-done | bytes 98328
  1.5 0.0 copy-start.1
  1.5 0.9 %copy-done.1 = f32[24,1024]{1,0:T(8,128)S(1)} copy-done((f32[24,1024]{1,0:T(8,128)S(1)}, f32[24,1024]{1,0:T(8,128)}, u32[]{:S(2)}) %copy-start.1) | copy-done | bytes 98328
  2.4 0.0 copy-start.2
  2.4 0.9 %copy-done.2 = s32[1,24,1024]{2,1,0:T(8,128)S(1)} copy-done((s32[1,24,1024]{2,1,0:T(8,128)S(1)}, s32[1,24,1024]{2,1,0:T(8,128)}, u32[]{:S(2)}) %copy-start.2) | copy-done | bytes 98328
  3.3 45.5 %shard_map.50 = (f32[9,24,1024]{2,1,0:T(8,128)S(1)}, f32[24,1024]{1,0:T(8,128)S(1)}, f32[24,1024]{1,0:T(8,128)S(1)}) custom-call(f32[24,1024]{1,0:T(8,128)S(1)} %copy-done, f32[24,1024]{1,0:T(8,128)S(1)} %copy-done.1, s32[1,24,1024]{2,1,0:T(8,128)S(1)} %copy-done.2), custom_call_target="tpu_custom_call" | custom-call | tf_op jit(solution)/shard_map/pallas_call | solution.py:290
  48.8 1.0 %multiply_bitcast_fusion = f32[1,9,24,1024]{3,2,1,0:T(8,128)} fusion(f32[9,24,1024]{2,1,0:T(8,128)S(1)} %get-tuple-element.5, f32[24,1024]{1,0:T(8,128)S(1)} %get-tuple-element.6), kind=kLoop, calls=%fused_computation | loop fusion | flops 221184 | bytes 1867776 | tf_op jit(solution)/shard_map/broadcast_in_dim | solution.py:318
  49.8 0.6 %copy.6 = f32[24,1024]{1,0:T(8,128)} copy(f32[24,1024]{1,0:T(8,128)S(1)} %get-tuple-element.11) | data formatting | bytes 196608
Async XLA Ops:
  0.6 0.9 %copy-start = (f32[24,1024]{1,0:T(8,128)S(1)}, f32[24,1024]{1,0:T(8,128)}, u32[]{:S(2)}) copy-start(f32[24,1024]{1,0:T(8,128)} %density_in.1) | copy-start | bytes 294916
  1.5 0.9 %copy-start.1 = (f32[24,1024]{1,0:T(8,128)S(1)}, f32[24,1024]{1,0:T(8,128)}, u32[]{:S(2)}) copy-start(f32[24,1024]{1,0:T(8,128)} %relax_in.1) | copy-start | bytes 294916
  2.4 0.9 %copy-start.2 = (s32[1,24,1024]{2,1,0:T(8,128)S(1)}, s32[1,24,1024]{2,1,0:T(8,128)}, u32[]{:S(2)}) copy-start(s32[1,24,1024]{2,1,0:T(8,128)} %pert_in.1) | copy-start | bytes 294916
where the time goes:
time: 50.7 us; the launch traced here: 50.5 us
  Pallas kernels  45.5 us (90%)
  local copies, waits for them, and re-layouts  3.31 us (7%)
  other arithmetic  1.01 us (2%)
  between operations  0.65 us (1%)
    pallas_call x1, Pallas kernels, on_device(): pl.pallas_call(functools.partial(kernel, ens, slabs), out_shape=(jax.Shap...  45.5 us
    unnamed x7, local copies, waits for them, and re-layouts  3.31 us
    broadcast_in_dim x1, other arithmetic, on_device(): return (lifted[None], projected)  1.01 us

commit v1 on v0

v1 whole, which is shorter than its diff:
```python
import functools

import jax
import jax.numpy as jnp
from jax import lax
from jax.experimental import pallas as pl
from jax.experimental.pallas import tpu as pltpu
from jax.sharding import PartitionSpec as P

MICRO_SPELLS = 3
STEPS = 8
TOTAL = MICRO_SPELLS * STEPS
LANES = 128
TILE = 8
WIDE = 4

row_moves = (0, 0, 1, 0, -1, 1, 1, -1, -1)
col_moves = (0, 1, 0, -1, 0, 1, -1, -1, 1)
mirrored = (0, 1, 4, 3, 2, 8, 7, 6, 5)
lattice_weights = (4.0 / 9.0,) + (1.0 / 9.0,) * 4 + (1.0 / 36.0,) * 4
shift_amp = 0.08
step_cap = 0.25
MESH = pl.DeviceIdType.MESH
OWN, NEAR, FAR = 0, 1, 2
DUMMY = MICRO_SPELLS


def collide(f, keep, third, ninth):
    plus = f[1] + (f[5] + f[8])
    minus = f[3] + (f[6] + f[7])
    density = (f[0] + (f[2] + f[4])) + (plus + minus)
    mom_col = plus - minus
    mom_row = (f[2] - f[4]) + ((f[5] + f[6]) - (f[7] + f[8]))
    inverse = 1.5 / density
    vel_row = mom_row * inverse
    vel_col = mom_col * inverse
    third_row = third * mom_row
    third_col = third * mom_col
    half_rr = third_row * vel_row
    half_cc = third_col * vel_col
    quarter_rc = (third_row * vel_col) * 0.5
    squares = half_rr + half_cc
    base = ninth * density - squares * (1.0 / 3.0)
    even_col = base + half_cc
    even_row = base + half_rr
    corner = 0.25 * (base + squares)
    even_57 = corner + quarter_rc
    even_68 = corner - quarter_rc
    odd_57 = 0.25 * (third_row + third_col)
    odd_68 = 0.25 * (third_row - third_col)
    out = (
        keep * f[0] + 4.0 * base,
        keep * f[1] + (even_col + third_col),
        keep * f[2] + (even_row + third_row),
        keep * f[3] + (even_col - third_col),
        keep * f[4] + (even_row - third_row),
        keep * f[5] + (even_57 + odd_57),
        keep * f[6] + (even_68 + odd_68),
        keep * f[7] + (even_57 - odd_57),
        keep * f[8] + (even_68 - odd_68),
    )
    return out, density


def kernel(
    ens,
    slabs,
    density_hbm,
    relax_hbm,
    pert_hbm,
    finals,
    scale_out,
    projected_out,
    density_in,
    pert_in,
    raws,
    even,
    odd,
    coef,
    gathered,
    change_at,
    fitted_at,
    squares,
    in_sem,
    halo_send,
    halo_recv,
    ens_send,
    ens_recv,
    sq_send,
    sq_recv,
):
    height, width = density_in.shape
    blocks = width // LANES
    chunks = height // TILE
    wide = WIDE if blocks % WIDE == 0 else 1
    me_e = lax.axis_index("ens")
    me_s = lax.axis_index("slab")
    flipped = lax.rem(me_s, 2)

    barrier = pltpu.get_barrier_semaphore()
    for k in range(1, ens):
        pl.semaphore_signal(
            barrier, inc=1, device_id={"ens": lax.rem(me_e + k, ens)}, device_id_type=MESH
        )
    for k in range(1, slabs):
        pl.semaphore_signal(
            barrier, inc=1, device_id={"slab": lax.rem(me_s + k, slabs)}, device_id_type=MESH
        )

    loads = [
        pltpu.make_async_copy(density_hbm, density_in, in_sem.at[0]),
        pltpu.make_async_copy(pert_hbm.at[0], pert_in, in_sem.at[1]),
        pltpu.make_async_copy(relax_hbm, raws.at[OWN, 1], in_sem.at[2]),
    ]
    for copy in loads:
        copy.start()

    lane = lax.broadcasted_iota(jnp.int32, (TILE, LANES), 1)
    sublane = lax.broadcasted_iota(jnp.int32, (TILE, LANES), 0)
    order = jnp.where(flipped == 1, TILE - 1 - sublane, sublane)
    edges = {1: lane == 0, -1: lane == LANES - 1}
    bodies = {1: lane != 0, -1: lane != LANES - 1}

    def flip(x):
        return jnp.take_along_axis(x, order, axis=0, mode="promise_in_bounds")

    def natural(c):
        return pl.multiple_of(TILE * jnp.where(flipped == 1, chunks - 1 - c, c), TILE)

    def moved_store(ref, at, first, x, move):
        count = x.shape[0]
        over = lambda mask, n: jnp.broadcast_to(mask[None], (n, TILE, LANES))
        turned = pltpu.roll(x, 1 if move == 1 else LANES - 1, 2)
        pltpu.store(
            ref.at[pl.ds(first, count), at, :], turned, mask=over(bodies[move], count)
        )
        edge = edges[move]
        low = first + move
        if low < 0:
            pltpu.store(ref.at[pl.ds(blocks - 1, 1), at, :], turned[:1], mask=over(edge, 1))
            turned, low, count = turned[1:], 0, count - 1
        elif low + count > blocks:
            pltpu.store(ref.at[pl.ds(0, 1), at, :], turned[count - 1 :], mask=over(edge, 1))
            turned, count = turned[: count - 1], count - 1
        if count:
            pltpu.store(ref.at[pl.ds(low, count), at, :], turned, mask=over(edge, count))

    def fill(place, offset):
        def body(c, carry):
            at = pl.ds(offset + c * TILE, TILE)
            rows = pl.ds(natural(c), TILE)
            for b in range(blocks):
                cols = slice(b * LANES, (b + 1) * LANES)
                rate = flip(raws[place, 1, rows, cols])
                fresh = flip(raws[place, 0, rows, cols])
                coef[0, b, at, :] = 1.0 - rate
                coef[1, b, at, :] = rate * (1.0 / 3.0)
                coef[2, b, at, :] = rate * (1.0 / 9.0)
                for weight, members in (
                    (lattice_weights[0], (0,)),
                    (lattice_weights[1], (1, 2, 3, 4)),
                    (lattice_weights[5], (5, 6, 7, 8)),
                ):
                    part = weight * fresh
                    for i in members:
                        if col_moves[i] == 0:
                            odd[i, b, at, :] = part
                        else:
                            moved_store(odd.at[i], at, b, part[None], col_moves[i])
            return carry

        lax.fori_loop(0, chunks, body, 0)

    front = height

    def group(k, low, slot=None):
        source, dest = (odd, even) if k % 2 == 0 else (even, odd)
        at = front + low
        rows = pl.ds(at, TILE)
        for first in range(0, blocks, wide):
            cols = pl.ds(first, wide)
            f = [source[i, cols, pl.ds(at - row_moves[i], TILE), :] for i in range(9)]
            out, density = collide(f, *(coef[n, cols, rows, :] for n in range(3)))
            if slot is not None:
                gathered[slot, me_e, cols, rows, :] = density
            for i in range(9):
                if col_moves[i] == 0:
                    dest[i, cols, rows, :] = out[i]
                else:
                    moved_store(dest.at[i], rows, first, out[i], col_moves[i])

    for copy in loads:
        copy.wait()
    for c in range(chunks):
        rows = slice(c * TILE, (c + 1) * TILE)
        raws[OWN, 0, rows, :] = density_in[rows, :] + shift_amp * pert_in[rows, :].astype(
            jnp.float32
        )
    fill(OWN, front)

    def triangle(k):
        low, high = k - 1, height + 1 - k
        for first in range(low, high, TILE):
            group(k, min(first, high - TILE), 0 if k == STEPS + 1 else None)

    triangle(2)
    pl.semaphore_wait(barrier, ens + slabs - 2)
    near_to = me_s + 1 - 2 * flipped
    far_to = lax.rem(me_s + slabs - 1 + 2 * flipped, slabs)
    halos = {}
    for place, target in ((FAR, far_to), (NEAR, near_to)):
        halos[place] = [
            pltpu.make_async_remote_copy(
                src_ref=raws.at[OWN, n],
                dst_ref=raws.at[place, n],
                send_sem=halo_send.at[place - 1, n],
                recv_sem=halo_recv.at[place - 1, n],
                device_id={"slab": target},
                device_id_type=MESH,
            )
            for n in (1, 0)
        ]
        for copy in halos[place]:
            copy.start()
    for k in range(3, STEPS + 2):
        triangle(k)

    for copy in halos[NEAR]:
        copy.wait_recv()
    fill(NEAR, front + height)

    def lean(t, carry):
        for n in range(4):
            k = 2 + 4 * t + n
            for j in range(chunks - 1, -1, -1):
                slot = jnp.where(t == 1, 0, DUMMY) if n == 3 else None
                group(n % 2, height + 1 - k + TILE * j, slot)
        return carry

    lax.fori_loop(0, 2, lean, 0)
    for k in range(STEPS + 2, TOTAL + 1):
        count = 2 * height + 2 - 2 * k
        for j in range((count + TILE - 1) // TILE - 1, -1, -1):
            group(k, k - 1 + TILE * j, 1 if k == 2 * STEPS + 1 else None)

    for copy in halos[FAR]:
        copy.wait_recv()
    fill(FAR, front - height)

    def strips(t, carry):
        for n in range(4):
            k = 2 + 4 * t + n
            for j in range(1, chunks + 1):
                slot = None
                if n == 3:
                    slot = jnp.where(t == 1, 0, jnp.where(t == 3, 1, DUMMY))
                group(n % 2, k - 1 - TILE * j, slot)
        return carry

    def send_spell(spell):
        copies = []
        own = pl.ds(front, height)
        for k in range(1, ens):
            copies.append(
                pltpu.make_async_remote_copy(
                    src_ref=gathered.at[spell, me_e, :, own],
                    dst_ref=gathered.at[spell, me_e, :, own],
                    send_sem=ens_send.at[spell, k - 1],
                    recv_sem=ens_recv.at[spell, k - 1],
                    device_id={"ens": lax.rem(me_e + k, ens)},
                    device_id_type=MESH,
                )
            )
        for copy in copies:
            copy.start()
        return copies

    lax.fori_loop(0, 2, strips, 0)
    sent = [send_spell(0)]
    lax.fori_loop(2, 4, strips, 0)
    sent.append(send_spell(1))
    for k in range(2 * STEPS + 2, TOTAL + 1):
        for j in range(1, chunks + 1):
            group(k, k - 1 - TILE * j)

    last = even if TOTAL % 2 == 0 else odd

    def settle(c, carry):
        at = front + c * TILE
        for b in range(blocks):
            total = last[0, b, pl.ds(at, TILE), :]
            for i in range(1, 9):
                total = total + last[i, b, pl.ds(at - row_moves[i], TILE), :]
            gathered[MICRO_SPELLS - 1, me_e, b, pl.ds(at, TILE), :] = total
        return carry

    lax.fori_loop(0, chunks, settle, 0)
    sent.append(send_spell(MICRO_SPELLS - 1))

    def put_finals(c, carry):
        at = front + c * TILE
        rows = pl.ds(natural(c), TILE)
        for i in range(9):
            to = jnp.where(flipped == 1, mirrored[i], i)
            for b in range(blocks):
                cols = slice(b * LANES, (b + 1) * LANES)
                finals[to, rows, cols] = flip(last[i, b, pl.ds(at - row_moves[i], TILE), :])
        return carry

    lax.fori_loop(0, chunks, put_finals, 0)

    for copies in sent:
        for copy in copies:
            copy.wait_recv()

    def mean(spell, at):
        total = gathered[spell, 0, :, at, :]
        for member in range(1, ens):
            total = total + gathered[spell, member, :, at, :]
        return total * (1.0 / ens)

    def fit(c, acc):
        at = pl.ds(front + c * TILE, TILE)
        to = pl.ds(pl.multiple_of(c * TILE, TILE), TILE)
        first, middle, final = (mean(spell, at) for spell in range(MICRO_SPELLS))
        change = final - first
        change_at[:, to, :] = change
        fitted_at[:, to, :] = (first + middle + final) * (1.0 / 3.0) + 0.5 * change
        return acc + jnp.sum(change * change, axis=0)

    acc = lax.fori_loop(0, chunks, fit, jnp.zeros((TILE, LANES), jnp.float32))
    squares[me_s] = acc
    copies = []
    for k in range(1, slabs):
        copies.append(
            pltpu.make_async_remote_copy(
                src_ref=squares.at[me_s],
                dst_ref=squares.at[me_s],
                send_sem=sq_send.at[k - 1],
                recv_sem=sq_recv.at[k - 1],
                device_id={"slab": lax.rem(me_s + k, slabs)},
                device_id_type=MESH,
            )
        )
    for copy in copies:
        copy.start()
    for copy in copies:
        copy.wait_recv()
    total = jnp.sum(jnp.sum(squares[...], axis=0), axis=(0, 1), keepdims=True)
    mean_square = total * (1.0 / (height * width * slabs))
    gain = step_cap / jnp.sqrt(mean_square + 1e-06)

    def project(c, carry):
        at = pl.ds(front + c * TILE, TILE)
        here = pl.ds(pl.multiple_of(c * TILE, TILE), TILE)
        rows = pl.ds(natural(c), TILE)
        for b in range(blocks):
            cols = slice(b * LANES, (b + 1) * LANES)
            projected = fitted_at[b, here, :] + gain * change_at[b, here, :]
            projected_out[rows, cols] = flip(projected)
            scale_out[rows, cols] = flip(
                projected / gathered[MICRO_SPELLS - 1, me_e, b, at, :]
            )
        return carry

    lax.fori_loop(0, chunks, project, 0)

    for group_of in [halos[NEAR], halos[FAR], copies] + sent:
        for copy in group_of:
            copy.wait_send()


def on_device(density0, relax_rate, perturbation):
    height, width = density0.shape
    ens, slabs = lax.axis_size("ens"), lax.axis_size("slab")
    assert perturbation.shape[0] == 1 and width % LANES == 0
    assert height == TOTAL and height % TILE == 0 and slabs % 2 == 0
    blocks = width // LANES
    rows = 3 * height
    f32 = jnp.float32
    field = jax.ShapeDtypeStruct((height, width), f32)
    vmem = pl.BlockSpec(memory_space=pltpu.VMEM)
    dma = pltpu.SemaphoreType.DMA
    finals, scale, projected = pl.pallas_call(
        functools.partial(kernel, ens, slabs),
        out_shape=(
            jax.ShapeDtypeStruct((9, height, width), f32),
            field,
            field,
        ),
        in_specs=[pl.BlockSpec(memory_space=pltpu.HBM)] * 3,
        out_specs=[vmem] * 3,
        scratch_shapes=[
            pltpu.VMEM((height, width), f32),
            pltpu.VMEM((height, width), jnp.int32),
            pltpu.VMEM((3, 2, height, width), f32),
            pltpu.VMEM((9, blocks, rows, LANES), f32),
            pltpu.VMEM((9, blocks, rows, LANES), f32),
            pltpu.VMEM((3, blocks, rows, LANES), f32),
            pltpu.VMEM((MICRO_SPELLS + 1, ens, blocks, rows, LANES), f32),
            pltpu.VMEM((blocks, height, LANES), f32),
            pltpu.VMEM((blocks, height, LANES), f32),
            pltpu.VMEM((slabs, TILE, LANES), f32),
            dma((3,)),
            dma((2, 2)),
            dma((2, 2)),
            dma((MICRO_SPELLS, ens - 1)),
            dma((MICRO_SPELLS, ens - 1)),
            dma((slabs - 1,)),
            dma((slabs - 1,)),
        ],
        compiler_params=pltpu.CompilerParams(
            collective_id=0, has_side_effects=True, vmem_limit_bytes=48 << 20
        ),
    )(density0, relax_rate, perturbation)
    lifted = finals * scale[None]
    return (lifted[None], projected)


def solution(mesh):
    in_specs = (P("slab", None), P("slab", None), P("ens", "slab", None))
    out_specs = (P("ens", None, "slab", None), P("slab", None))
    return jax.shard_map(
        on_device, mesh=mesh, in_specs=in_specs, out_specs=out_specs, check_vma=False
    )
```

time: 50.7 us -> 38.8 us (0.77)
  Pallas kernels: 45.5 us -> 33.6 us
    pallas_call x1, Pallas kernels: 45.5 us -> 33.6 us  [on_device(): pl.pallas_call(functools.partial(kernel, ens, slabs), out_shape=(jax.Shap...]
where the time goes in v1:
time: 38.8 us; the launch traced here: 38.6 us
  Pallas kernels  33.6 us (87%)
  local copies, waits for them, and re-layouts  3.31 us (9%)
  other arithmetic  1.01 us (3%)
  between operations  0.65 us (2%)
    pallas_call x1, Pallas kernels, on_device(): pl.pallas_call(functools.partial(kernel, ens, slabs), out_shape=(jax.Shap...  33.6 us
    unnamed x7, local copies, waits for them, and re-layouts  3.31 us
    broadcast_in_dim x1, other arithmetic, on_device(): return (lifted[None], projected)  1.01 us

profile of v1, /device:TPU:0, one launch (start us, length us, event | category | flops | bytes accessed | tf_op | source)
XLA Modules:
  0.0 38.6 jit_solution(15932023839586931382)
XLA Ops:
  0.6 0.0 copy-start
  0.6 0.9 %copy-done = f32[24,1024]{1,0:T(8,128)S(1)} copy-done((f32[24,1024]{1,0:T(8,128)S(1)}, f32[24,1024]{1,0:T(8,128)}, u32[]{:S(2)}) %copy-start) | copy-done | bytes 98328
  1.5 0.0 copy-start.1
  1.5 0.9 %copy-done.1 = f32[24,1024]{1,0:T(8,128)S(1)} copy-done((f32[24,1024]{1,0:T(8,128)S(1)}, f32[24,1024]{1,0:T(8,128)}, u32[]{:S(2)}) %copy-start.1) | copy-done | bytes 98328
  2.4 0.0 copy-start.2
  2.4 0.9 %copy-done.2 = s32[1,24,1024]{2,1,0:T(8,128)S(1)} copy-done((s32[1,24,1024]{2,1,0:T(8,128)S(1)}, s32[1,24,1024]{2,1,0:T(8,128)}, u32[]{:S(2)}) %copy-start.2) | copy-done | bytes 98328
  3.3 33.6 %shard_map.50 = (f32[9,24,1024]{2,1,0:T(8,128)S(1)}, f32[24,1024]{1,0:T(8,128)S(1)}, f32[24,1024]{1,0:T(8,128)S(1)}) custom-call(f32[24,1024]{1,0:T(8,128)S(1)} %copy-done, f32[24,1024]{1,0:T(8,128)S(1)} %copy-done.1, s32[1,24,1024]{2,1,0:T(8,128)S(1)} %copy-done.2), custom_call_target="tpu_custom_call" | custom-call | tf_op jit(solution)/shard_map/pallas_call | solution.py:384
  36.9 1.0 %multiply_bitcast_fusion = f32[1,9,24,1024]{3,2,1,0:T(8,128)} fusion(f32[9,24,1024]{2,1,0:T(8,128)S(1)} %get-tuple-element.5, f32[24,1024]{1,0:T(8,128)S(1)} %get-tuple-element.6), kind=kLoop, calls=%fused_computation | loop fusion | flops 221184 | bytes 1867776 | tf_op jit(solution)/shard_map/broadcast_in_dim | solution.py:417
  37.9 0.6 %copy.6 = f32[24,1024]{1,0:T(8,128)} copy(f32[24,1024]{1,0:T(8,128)S(1)} %get-tuple-element.11) | data formatting | bytes 196608
Async XLA Ops:
  0.6 0.9 %copy-start = (f32[24,1024]{1,0:T(8,128)S(1)}, f32[24,1024]{1,0:T(8,128)}, u32[]{:S(2)}) copy-start(f32[24,1024]{1,0:T(8,128)} %density_hbm.1) | copy-start | bytes 294916
  1.5 0.9 %copy-start.1 = (f32[24,1024]{1,0:T(8,128)S(1)}, f32[24,1024]{1,0:T(8,128)}, u32[]{:S(2)}) copy-start(f32[24,1024]{1,0:T(8,128)} %relax_hbm.1) | copy-start | bytes 294916
  2.4 0.9 %copy-start.2 = (s32[1,24,1024]{2,1,0:T(8,128)S(1)}, s32[1,24,1024]{2,1,0:T(8,128)}, u32[]{:S(2)}) copy-start(s32[1,24,1024]{2,1,0:T(8,128)} %pert_hbm.1) | copy-start | bytes 294916

commit v2 on v1

--- a/solution.py
+++ b/solution.py
@@ -22,7 +22,8 @@
 step_cap = 0.25
 MESH = pl.DeviceIdType.MESH
 OWN, NEAR, FAR = 0, 1, 2
-DUMMY = MICRO_SPELLS
+DUMMY = MICRO_SPELLS - 1
+PIECES = 5
 
 
 def collide(f, keep, third, ninth):
@@ -78,14 +79,20 @@
     odd,
     coef,
     gathered,
+    partial,
+    received,
     change_at,
     fitted_at,
     squares,
     in_sem,
-    halo_send,
-    halo_recv,
+    near_send,
+    near_recv,
+    far_send,
+    far_recv,
     ens_send,
     ens_recv,
+    pair_send,
+    pair_recv,
     sq_send,
     sq_recv,
 ):
@@ -93,6 +100,7 @@
     blocks = width // LANES
     chunks = height // TILE
     wide = WIDE if blocks % WIDE == 0 else 1
+    phases = ens.bit_length() - 1
     me_e = lax.axis_index("ens")
     me_s = lax.axis_index("slab")
     flipped = lax.rem(me_s, 2)
@@ -145,8 +153,8 @@
         if count:
             pltpu.store(ref.at[pl.ds(low, count), at, :], turned, mask=over(edge, count))
 
-    def fill(place, offset):
-        def body(c, carry):
+    def fill(place, offset, which):
+        for c in which:
             at = pl.ds(offset + c * TILE, TILE)
             rows = pl.ds(natural(c), TILE)
             for b in range(blocks):
@@ -167,9 +175,6 @@
                             odd[i, b, at, :] = part
                         else:
                             moved_store(odd.at[i], at, b, part[None], col_moves[i])
-            return carry
-
-        lax.fori_loop(0, chunks, body, 0)
 
     front = height
 
@@ -196,7 +201,7 @@
         raws[OWN, 0, rows, :] = density_in[rows, :] + shift_amp * pert_in[rows, :].astype(
             jnp.float32
         )
-    fill(OWN, front)
+    fill(OWN, front, range(chunks))
 
     def triangle(k):
         low, high = k - 1, height + 1 - k
@@ -204,98 +209,143 @@
             group(k, min(first, high - TILE), 0 if k == STEPS + 1 else None)
 
     triangle(2)
+    triangle(3)
     pl.semaphore_wait(barrier, ens + slabs - 2)
     near_to = me_s + 1 - 2 * flipped
     far_to = lax.rem(me_s + slabs - 1 + 2 * flipped, slabs)
-    halos = {}
-    for place, target in ((FAR, far_to), (NEAR, near_to)):
-        halos[place] = [
+    far = []
+    for c in range(chunks):
+        rows = pl.ds(natural(c), TILE)
+        far.append(
             pltpu.make_async_remote_copy(
-                src_ref=raws.at[OWN, n],
-                dst_ref=raws.at[place, n],
-                send_sem=halo_send.at[place - 1, n],
-                recv_sem=halo_recv.at[place - 1, n],
-                device_id={"slab": target},
+                src_ref=raws.at[OWN, :, rows],
+                dst_ref=raws.at[FAR, :, rows],
+                send_sem=far_send.at[c],
+                recv_sem=far_recv.at[c],
+                device_id={"slab": far_to},
                 device_id_type=MESH,
             )
-            for n in (1, 0)
-        ]
-        for copy in halos[place]:
-            copy.start()
-    for k in range(3, STEPS + 2):
+        )
+    near = pltpu.make_async_remote_copy(
+        src_ref=raws.at[OWN],
+        dst_ref=raws.at[NEAR],
+        send_sem=near_send,
+        recv_sem=near_recv,
+        device_id={"slab": near_to},
+        device_id_type=MESH,
+    )
+    near.start()
+    for copy in far:
+        copy.start()
+    for k in range(4, STEPS + 2):
         triangle(k)
 
-    for copy in halos[NEAR]:
-        copy.wait_recv()
-    fill(NEAR, front + height)
-
-    def lean(t, carry):
+    near.wait_recv()
+    fill(NEAR, front + height, range(chunks))
+
+    def lean(t, base):
         for n in range(4):
-            k = 2 + 4 * t + n
-            for j in range(chunks - 1, -1, -1):
+            for j in range(chunks):
                 slot = jnp.where(t == 1, 0, DUMMY) if n == 3 else None
-                group(n % 2, height + 1 - k + TILE * j, slot)
-        return carry
-
-    lax.fori_loop(0, 2, lean, 0)
-    for k in range(STEPS + 2, TOTAL + 1):
-        count = 2 * height + 2 - 2 * k
-        for j in range((count + TILE - 1) // TILE - 1, -1, -1):
-            group(k, k - 1 + TILE * j, 1 if k == 2 * STEPS + 1 else None)
-
-    for copy in halos[FAR]:
-        copy.wait_recv()
-    fill(FAR, front - height)
-
-    def strips(t, carry):
-        for n in range(4):
-            k = 2 + 4 * t + n
-            for j in range(1, chunks + 1):
-                slot = None
-                if n == 3:
-                    slot = jnp.where(t == 1, 0, jnp.where(t == 3, 1, DUMMY))
-                group(n % 2, k - 1 - TILE * j, slot)
-        return carry
-
-    def send_spell(spell):
+                group(n % 2, base + (TILE * j - n), slot)
+        return base - 4
+
+    sent = []
+
+    def send(spell, low, high):
+        own = pl.ds(front + low, high - low)
+        piece = len(sent)
         copies = []
-        own = pl.ds(front, height)
         for k in range(1, ens):
             copies.append(
                 pltpu.make_async_remote_copy(
                     src_ref=gathered.at[spell, me_e, :, own],
                     dst_ref=gathered.at[spell, me_e, :, own],
-                    send_sem=ens_send.at[spell, k - 1],
-                    recv_sem=ens_recv.at[spell, k - 1],
+                    send_sem=ens_send.at[piece, k - 1],
+                    recv_sem=ens_recv.at[piece, k - 1],
                     device_id={"ens": lax.rem(me_e + k, ens)},
                     device_id_type=MESH,
                 )
             )
         for copy in copies:
             copy.start()
-        return copies
-
-    lax.fori_loop(0, 2, strips, 0)
-    sent = [send_spell(0)]
-    lax.fori_loop(2, 4, strips, 0)
-    sent.append(send_spell(1))
-    for k in range(2 * STEPS + 2, TOTAL + 1):
-        for j in range(1, chunks + 1):
-            group(k, k - 1 - TILE * j)
+        sent.append(copies)
+
+    def near_side(k):
+        count = 2 * height + 2 - 2 * k
+        for j in range((count + TILE - 1) // TILE - 1, -1, -1):
+            group(k, k - 1 + TILE * j, sample.get(k))
+
+    def strip(m, k):
+        if 2 <= k <= TOTAL:
+            group(k, k - 1 - TILE * m, sample.get(k))
+
+    def arrived(c):
+        far[c].wait_recv()
+        fill(FAR, front - height, (chunks - 1 - c,))
+
+    def settle(b, c):
+        at = front + c * TILE
+        total = last[0, b, pl.ds(at, TILE), :]
+        for i in range(1, 9):
+            total = total + last[i, b, pl.ds(at - row_moves[i], TILE), :]
+        return total
+
+    cuts = [blocks * p // phases for p in range(phases + 1)]
+
+    def pair(n, q, p):
+        stride = 2 ** ((p + q) % phases)
+        peer = me_e + stride - 2 * stride * lax.rem(me_e // stride, 2)
+        part = pl.ds(cuts[p], cuts[p + 1] - cuts[p])
+        return pltpu.make_async_remote_copy(
+            src_ref=partial.at[n, q, part],
+            dst_ref=received.at[n, q, part],
+            send_sem=pair_send.at[n, q, p],
+            recv_sem=pair_recv.at[n, q, p],
+            device_id={"ens": peer},
+            device_id_type=MESH,
+        )
+
+    pairs = [[[pair(n, q, p) for p in range(phases)] for q in range(phases)] for n in range(3)]
+
+    def send_pairs(n, c):
+        for b in range(blocks):
+            partial[n, 0, b] = settle(b, c)
+        for copy in pairs[n][0]:
+            copy.start()
 
     last = even if TOTAL % 2 == 0 else odd
-
-    def settle(c, carry):
-        at = front + c * TILE
-        for b in range(blocks):
-            total = last[0, b, pl.ds(at, TILE), :]
-            for i in range(1, 9):
-                total = total + last[i, b, pl.ds(at - row_moves[i], TILE), :]
-            gathered[MICRO_SPELLS - 1, me_e, b, pl.ds(at, TILE), :] = total
-        return carry
-
-    lax.fori_loop(0, chunks, settle, 0)
-    sent.append(send_spell(MICRO_SPELLS - 1))
+    sample = {STEPS + 1: 0, 2 * STEPS + 1: 1}
+    lax.fori_loop(0, 2, lean, height - 1)
+    send(0, STEPS, height)
+    for k in range(STEPS + 2, STEPS + 5):
+        near_side(k)
+    arrived(0)
+    for n in range(TOTAL + 10):
+        if n == 7:
+            send(1, 2 * STEPS, height)
+            arrived(1)
+        if n == 11:
+            send(0, 0, STEPS)
+            arrived(2)
+        if n == 16:
+            send(1, STEPS, 2 * STEPS)
+        if n == 23:
+            for b in range(blocks):
+                partial[2, 0, b] = gathered[1, me_e, b, pl.ds(front, TILE), :]
+            send_pairs(0, 2)
+            for copy in pairs[2][0]:
+                copy.start()
+        if n == 30:
+            send_pairs(1, 1)
+        if STEPS + 5 + n <= TOTAL:
+            near_side(STEPS + 5 + n)
+        strip(1, n + 2)
+        strip(2, n - 5)
+        strip(3, n - 9)
+    for b in range(blocks):
+        gathered[MICRO_SPELLS - 1, me_e, b, pl.ds(front, TILE), :] = settle(b, 0)
+    send(MICRO_SPELLS - 1, 0, TILE)
 
     def put_finals(c, carry):
         at = front + c * TILE
@@ -309,26 +359,65 @@
 
     lax.fori_loop(0, chunks, put_finals, 0)
 
-    for copies in sent:
+    def direct(spell, b, low, count):
+        at = pl.ds(front + low, count)
+        total = gathered[spell, 0, b, at, :]
+        for member in range(1, ens):
+            total = total + gathered[spell, member, b, at, :]
+        return total * (1.0 / ens)
+
+    def paired(n, b):
+        return (partial[n, phases - 1, b] + received[n, phases - 1, b]) * (1.0 / ens)
+
+    def pass_on(n):
+        for q in range(phases - 1):
+            for p in range(phases):
+                part = slice(cuts[p], cuts[p + 1])
+                pairs[n][q][p].wait_recv()
+                partial[n, q + 1, part] = partial[n, q, part] + received[n, q, part]
+                pairs[n][q + 1][p].start()
+
+    def early(b, carry):
+        change_at[b] = direct(0, b, 0, height)
+        fitted_at[b, pl.ds(TILE, height - TILE), :] = direct(1, b, TILE, height - TILE)
+        return carry
+
+    pass_on(0)
+    for copies in sent[:-1]:
         for copy in copies:
             copy.wait_recv()
-
-    def mean(spell, at):
-        total = gathered[spell, 0, :, at, :]
-        for member in range(1, ens):
-            total = total + gathered[spell, member, :, at, :]
-        return total * (1.0 / ens)
-
-    def fit(c, acc):
-        at = pl.ds(front + c * TILE, TILE)
-        to = pl.ds(pl.multiple_of(c * TILE, TILE), TILE)
-        first, middle, final = (mean(spell, at) for spell in range(MICRO_SPELLS))
-        change = final - first
-        change_at[:, to, :] = change
-        fitted_at[:, to, :] = (first + middle + final) * (1.0 / 3.0) + 0.5 * change
-        return acc + jnp.sum(change * change, axis=0)
-
-    acc = lax.fori_loop(0, chunks, fit, jnp.zeros((TILE, LANES), jnp.float32))
+    lax.fori_loop(0, blocks, early, 0)
+    pass_on(2)
+    pass_on(1)
+    for copy in pairs[2][phases - 1]:
+        copy.wait_recv()
+    for b in range(blocks):
+        fitted_at[b, 0:TILE] = paired(2, b)
+    for b in range(blocks):
+        first = change_at[b]
+        fitted_at[b] = (first + fitted_at[b]) * (1.0 / 3.0) - 0.5 * first
+    acc = jnp.zeros((TILE, LANES), jnp.float32)
+
+    def fit(acc, b, c, final):
+        rows = slice(c * TILE, (c + 1) * TILE)
+        change = final - change_at[b, rows]
+        fitted_at[b, rows] = fitted_at[b, rows] + (1.0 / 3.0 + 0.5) * final
+        change_at[b, rows] = change
+        return acc + change * change
+
+    for n, c in ((0, 2), (None, 0), (1, 1)):
+        if n is None:
+            for copy in sent[-1]:
+                copy.wait_recv()
+        else:
+            for copy in pairs[n][phases - 1]:
+                copy.wait_recv()
+        for b in range(blocks):
+            if n is None:
+                final = direct(MICRO_SPELLS - 1, b, 0, TILE)
+            else:
+                final = paired(n, b)
+            acc = fit(acc, b, c, final)
     squares[me_s] = acc
     copies = []
     for k in range(1, slabs):
@@ -350,24 +439,34 @@
     mean_square = total * (1.0 / (height * width * slabs))
     gain = step_cap / jnp.sqrt(mean_square + 1e-06)
 
-    def project(c, carry):
-        at = pl.ds(front + c * TILE, TILE)
-        here = pl.ds(pl.multiple_of(c * TILE, TILE), TILE)
+    for c in range(chunks):
+        here = slice(c * TILE, (c + 1) * TILE)
         rows = pl.ds(natural(c), TILE)
         for b in range(blocks):
             cols = slice(b * LANES, (b + 1) * LANES)
+            if c == 0:
+                density = gathered[MICRO_SPELLS - 1, me_e, b, pl.ds(front, TILE), :]
+            else:
+                density = partial[2 - c, 0, b]
             projected = fitted_at[b, here, :] + gain * change_at[b, here, :]
             projected_out[rows, cols] = flip(projected)
-            scale_out[rows, cols] = flip(
-                projected / gathered[MICRO_SPELLS - 1, me_e, b, at, :]
-            )
-        return carry
-
-    lax.fori_loop(0, chunks, project, 0)
-
-    for group_of in [halos[NEAR], halos[FAR], copies] + sent:
+            scale_out[rows, cols] = flip(projected / density)
+
+    for group_of in [[near], far, copies] + sent + pairs[0] + pairs[1] + pairs[2]:
         for copy in group_of:
             copy.wait_send()
+
+
+def lift(finals, scale, projected, lifted_out, projected_out, scaled, sem):
+    copies = [pltpu.make_async_copy(projected, projected_out, sem.at[9])]
+    copies[0].start()
+    for i in range(9):
+        scaled[i] = finals[i] * scale[...]
+        copy = pltpu.make_async_copy(scaled.at[i], lifted_out.at[0, i], sem.at[i])
+        copy.start()
+        copies.append(copy)
+    for copy in copies:
+        copy.wait()
 
 
 def on_device(density0, relax_rate, perturbation):
@@ -377,9 +476,14 @@
     assert height == TOTAL and height % TILE == 0 and slabs % 2 == 0
     blocks = width // LANES
     rows = 3 * height
+    phases = ens.bit_length() - 1
+    assert ens == 2**phases
+    chunks = height // TILE
+    assert chunks == 3
     f32 = jnp.float32
     field = jax.ShapeDtypeStruct((height, width), f32)
     vmem = pl.BlockSpec(memory_space=pltpu.VMEM)
+    hbm = pl.BlockSpec(memory_space=pltpu.HBM)
     dma = pltpu.SemaphoreType.DMA
     finals, scale, projected = pl.pallas_call(
         functools.partial(kernel, ens, slabs),
@@ -388,7 +492,7 @@
             field,
             field,
         ),
-        in_specs=[pl.BlockSpec(memory_space=pltpu.HBM)] * 3,
+        in_specs=[hbm] * 3,
         out_specs=[vmem] * 3,
         scratch_shapes=[
             pltpu.VMEM((height, width), f32),
@@ -397,24 +501,36 @@
             pltpu.VMEM((9, blocks, rows, LANES), f32),
             pltpu.VMEM((9, blocks, rows, LANES), f32),
             pltpu.VMEM((3, blocks, rows, LANES), f32),
-            pltpu.VMEM((MICRO_SPELLS + 1, ens, blocks, rows, LANES), f32),
+            pltpu.VMEM((MICRO_SPELLS, ens, blocks, rows, LANES), f32),
+            pltpu.VMEM((3, phases, blocks, TILE, LANES), f32),
+            pltpu.VMEM((3, phases, blocks, TILE, LANES), f32),
             pltpu.VMEM((blocks, height, LANES), f32),
             pltpu.VMEM((blocks, height, LANES), f32),
             pltpu.VMEM((slabs, TILE, LANES), f32),
             dma((3,)),
-            dma((2, 2)),
-            dma((2, 2)),
-            dma((MICRO_SPELLS, ens - 1)),
-            dma((MICRO_SPELLS, ens - 1)),
+            dma(()),
+            dma(()),
+            dma((chunks,)),
+            dma((chunks,)),
+            dma((PIECES, ens - 1)),
+            dma((PIECES, ens - 1)),
+            dma((3, phases, phases)),
+            dma((3, phases, phases)),
             dma((slabs - 1,)),
             dma((slabs - 1,)),
         ],
         compiler_params=pltpu.CompilerParams(
             collective_id=0, has_side_effects=True, vmem_limit_bytes=48 << 20
         ),
-    )(density0, relax_rate, perturbation)
-    lifted = finals * scale[None]
-    return (lifted[None], projected)
+    )(*(pltpu.with_memory_space_constraint(x, pltpu.HBM) for x in (density0, relax_rate, perturbation)))
+    return pl.pallas_call(
+        lift,
+        out_shape=(jax.ShapeDtypeStruct((1, 9, height, width), f32), field),
+        in_specs=[vmem] * 3,
+        out_specs=[hbm] * 2,
+        scratch_shapes=[pltpu.VMEM((9, height, width), f32), dma((10,))],
+        compiler_params=pltpu.CompilerParams(vmem_limit_bytes=2 << 20),
+    )(finals, scale, projected)
 
 
 def solution(mesh):

time: 38.8 us -> 29.2 us (0.75)
  Pallas kernels: 33.6 us -> 28.4 us
  local copies, waits for them, and re-layouts: 3.31 us -> 0 us
  other arithmetic: 1.01 us -> 0 us
    pallas_call x1, Pallas kernels: 33.6 us -> 27.4 us  [on_device(): pl.pallas_call(functools.partial(kernel, ens, slabs), out_shape=(jax.Shap...]
    unnamed x7 -> x0, local copies, waits for them, and re-layouts: 3.31 us -> none
    pallas_call x0 -> x1, Pallas kernels: none -> 1.02 us  [on_device(): pl.pallas_call(lift, out_shape=(jax.ShapeDtypeStruct((1, 9, height, width...]
    broadcast_in_dim x1 -> x0, other arithmetic: 1.01 us -> none  [on_device(): return (lifted[None], projected)]
where the time goes in v2:
time: 29.2 us; the launch traced here: 29.1 us
  Pallas kernels  28.4 us (97%)
  between operations  0.64 us (2%)
    pallas_call x1, Pallas kernels, on_device(): pl.pallas_call(functools.partial(kernel, ens, slabs), out_shape=(jax.Shap...  27.4 us
    pallas_call x1, Pallas kernels, on_device(): pl.pallas_call(lift, out_shape=(jax.ShapeDtypeStruct((1, 9, height, width...  1.02 us

profile of v2, /device:TPU:0, one launch (start us, length us, event | category | flops | bytes accessed | tf_op | source)
XLA Modules:
  0.0 29.1 jit_solution(15777229929980508591)
XLA Ops:
  0.6 27.4 %shard_map.50 = (f32[9,24,1024]{2,1,0:T(8,128)S(1)}, f32[24,1024]{1,0:T(8,128)S(1)}, f32[24,1024]{1,0:T(8,128)S(1)}) custom-call(f32[24,1024]{1,0:T(8,128)} %density_hbm.1, f32[24,1024]{1,0:T(8,128)} %relax_hbm.1, s32[1,24,1024]{2,1,0:T(8,128)} %pert_hbm.1), custom_call_target="tpu_custom_call" | custom-call | tf_op jit(solution)/shard_map/pallas_call | solution.py:488
  28.0 1.0 %shard_map.51 = (f32[1,9,24,1024]{3,2,1,0:T(8,128)}, f32[24,1024]{1,0:T(8,128)}) custom-call(f32[9,24,1024]{2,1,0:T(8,128)S(1)} %get-tuple-element.5.finals, f32[24,1024]{1,0:T(8,128)S(1)} %get-tuple-element.6.scale, f32[24,1024]{1,0:T(8,128)S(1)} %get-tuple-element.7.projected), custom_call_target="tpu_custom_call" | custom-call | tf_op jit(solution)/shard_map/pallas_call | solution.py:526

commit v3 on v2

--- a/solution.py
+++ b/solution.py
@@ -23,7 +23,6 @@
 MESH = pl.DeviceIdType.MESH
 OWN, NEAR, FAR = 0, 1, 2
 DUMMY = MICRO_SPELLS - 1
-PIECES = 5
 
 
 def collide(f, keep, third, ninth):
@@ -85,14 +84,14 @@
     fitted_at,
     squares,
     in_sem,
-    near_send,
+    halo_send,
     near_recv,
-    far_send,
     far_recv,
     ens_send,
     ens_recv,
     pair_send,
-    pair_recv,
+    ahead_recv,
+    tail_recv,
     sq_send,
     sq_recv,
 ):
@@ -128,6 +127,9 @@
     order = jnp.where(flipped == 1, TILE - 1 - sublane, sublane)
     edges = {1: lane == 0, -1: lane == LANES - 1}
     bodies = {1: lane != 0, -1: lane != LANES - 1}
+
+    def drain(ref, sem):
+        pltpu.make_async_copy(ref, ref, sem).wait()
 
     def flip(x):
         return jnp.take_along_axis(x, order, axis=0, mode="promise_in_bounds")
@@ -220,7 +222,7 @@
             pltpu.make_async_remote_copy(
                 src_ref=raws.at[OWN, :, rows],
                 dst_ref=raws.at[FAR, :, rows],
-                send_sem=far_send.at[c],
+                send_sem=halo_send,
                 recv_sem=far_recv.at[c],
                 device_id={"slab": far_to},
                 device_id_type=MESH,
@@ -229,7 +231,7 @@
     near = pltpu.make_async_remote_copy(
         src_ref=raws.at[OWN],
         dst_ref=raws.at[NEAR],
-        send_sem=near_send,
+        send_sem=halo_send,
         recv_sem=near_recv,
         device_id={"slab": near_to},
         device_id_type=MESH,
@@ -250,26 +252,27 @@
                 group(n % 2, base + (TILE * j - n), slot)
         return base - 4
 
-    sent = []
+    def differing(mask):
+        peer = me_e
+        for n in range(phases):
+            if mask >> n & 1:
+                peer = peer + 2**n - 2 ** (n + 1) * lax.rem(me_e // 2**n, 2)
+        return peer
 
     def send(spell, low, high):
         own = pl.ds(front + low, high - low)
-        piece = len(sent)
-        copies = []
-        for k in range(1, ens):
-            copies.append(
-                pltpu.make_async_remote_copy(
-                    src_ref=gathered.at[spell, me_e, :, own],
-                    dst_ref=gathered.at[spell, me_e, :, own],
-                    send_sem=ens_send.at[piece, k - 1],
-                    recv_sem=ens_recv.at[piece, k - 1],
-                    device_id={"ens": lax.rem(me_e + k, ens)},
-                    device_id_type=MESH,
-                )
-            )
-        for copy in copies:
-            copy.start()
-        sent.append(copies)
+        for k in sorted(range(1, ens), key=lambda k: -k.bit_count()):
+            pltpu.make_async_remote_copy(
+                src_ref=gathered.at[spell, me_e, :, own],
+                dst_ref=gathered.at[spell, me_e, :, own],
+                send_sem=ens_send,
+                recv_sem=ens_recv.at[spell // (MICRO_SPELLS - 1)],
+                device_id={"ens": differing(k)},
+                device_id_type=MESH,
+            ).start()
+
+    def sent_bytes(rows):
+        return gathered.at[0, pl.ds(0, ens - 1), :, pl.ds(0, rows)]
 
     def near_side(k):
         count = 2 * height + 2 - 2 * k
@@ -294,14 +297,17 @@
     cuts = [blocks * p // phases for p in range(phases + 1)]
 
     def pair(n, q, p):
-        stride = 2 ** ((p + q) % phases)
-        peer = me_e + stride - 2 * stride * lax.rem(me_e // stride, 2)
+        peer = differing(2 ** ((p + q) % phases))
         part = pl.ds(cuts[p], cuts[p + 1] - cuts[p])
+        if n == 1:
+            arrival = tail_recv.at[min(q * phases + p, (phases - 1) * phases)]
+        else:
+            arrival = ahead_recv.at[q]
         return pltpu.make_async_remote_copy(
             src_ref=partial.at[n, q, part],
             dst_ref=received.at[n, q, part],
-            send_sem=pair_send.at[n, q, p],
-            recv_sem=pair_recv.at[n, q, p],
+            send_sem=pair_send,
+            recv_sem=arrival,
             device_id={"ens": peer},
             device_id_type=MESH,
         )
@@ -321,11 +327,11 @@
     for k in range(STEPS + 2, STEPS + 5):
         near_side(k)
     arrived(0)
-    for n in range(TOTAL + 10):
+    for n in range(TOTAL + 11):
         if n == 7:
             send(1, 2 * STEPS, height)
             arrived(1)
-        if n == 11:
+        if n == 12:
             send(0, 0, STEPS)
             arrived(2)
         if n == 16:
@@ -342,7 +348,7 @@
             near_side(STEPS + 5 + n)
         strip(1, n + 2)
         strip(2, n - 5)
-        strip(3, n - 9)
+        strip(3, n - 10)
     for b in range(blocks):
         gathered[MICRO_SPELLS - 1, me_e, b, pl.ds(front, TILE), :] = settle(b, 0)
     send(MICRO_SPELLS - 1, 0, TILE)
@@ -369,28 +375,30 @@
     def paired(n, b):
         return (partial[n, phases - 1, b] + received[n, phases - 1, b]) * (1.0 / ens)
 
-    def pass_on(n):
-        for q in range(phases - 1):
-            for p in range(phases):
-                part = slice(cuts[p], cuts[p + 1])
-                pairs[n][q][p].wait_recv()
-                partial[n, q + 1, part] = partial[n, q, part] + received[n, q, part]
-                pairs[n][q + 1][p].start()
+    def pass_on(q, n, p):
+        part = slice(cuts[p], cuts[p + 1])
+        partial[n, q + 1, part] = partial[n, q, part] + received[n, q, part]
+        pairs[n][q + 1][p].start()
+
+    ahead_bytes = partial.at[pl.ds(0, 2), 0]
 
     def early(b, carry):
         change_at[b] = direct(0, b, 0, height)
         fitted_at[b, pl.ds(TILE, height - TILE), :] = direct(1, b, TILE, height - TILE)
         return carry
 
-    pass_on(0)
-    for copies in sent[:-1]:
-        for copy in copies:
-            copy.wait_recv()
+    for q in range(phases - 1):
+        drain(ahead_bytes, ahead_recv.at[q])
+        for n in (0, 2):
+            for p in range(phases):
+                pass_on(q, n, p)
+    drain(sent_bytes(2 * height - TILE), ens_recv.at[0])
     lax.fori_loop(0, blocks, early, 0)
-    pass_on(2)
-    pass_on(1)
-    for copy in pairs[2][phases - 1]:
-        copy.wait_recv()
+    for q in range(phases - 1):
+        for p in range(phases):
+            pairs[1][q][p].wait_recv()
+            pass_on(q, 1, p)
+    drain(ahead_bytes, ahead_recv.at[phases - 1])
     for b in range(blocks):
         fitted_at[b, 0:TILE] = paired(2, b)
     for b in range(blocks):
@@ -407,38 +415,30 @@
 
     for n, c in ((0, 2), (None, 0), (1, 1)):
         if n is None:
-            for copy in sent[-1]:
-                copy.wait_recv()
-        else:
-            for copy in pairs[n][phases - 1]:
-                copy.wait_recv()
+            drain(sent_bytes(TILE), ens_recv.at[1])
+        if n == 1:
+            drain(partial.at[1, 0], tail_recv.at[(phases - 1) * phases])
         for b in range(blocks):
             if n is None:
                 final = direct(MICRO_SPELLS - 1, b, 0, TILE)
             else:
                 final = paired(n, b)
             acc = fit(acc, b, c, final)
-    squares[me_s] = acc
+    squares[me_s] = jnp.sum(acc, axis=0, keepdims=True)
     copies = []
     for k in range(1, slabs):
         copies.append(
             pltpu.make_async_remote_copy(
                 src_ref=squares.at[me_s],
                 dst_ref=squares.at[me_s],
-                send_sem=sq_send.at[k - 1],
-                recv_sem=sq_recv.at[k - 1],
+                send_sem=sq_send,
+                recv_sem=sq_recv,
                 device_id={"slab": lax.rem(me_s + k, slabs)},
                 device_id_type=MESH,
             )
         )
     for copy in copies:
         copy.start()
-    for copy in copies:
-        copy.wait_recv()
-    total = jnp.sum(jnp.sum(squares[...], axis=0), axis=(0, 1), keepdims=True)
-    mean_square = total * (1.0 / (height * width * slabs))
-    gain = step_cap / jnp.sqrt(mean_square + 1e-06)
-
     for c in range(chunks):
         here = slice(c * TILE, (c + 1) * TILE)
         rows = pl.ds(natural(c), TILE)
@@ -448,25 +448,33 @@
                 density = gathered[MICRO_SPELLS - 1, me_e, b, pl.ds(front, TILE), :]
             else:
                 density = partial[2 - c, 0, b]
-            projected = fitted_at[b, here, :] + gain * change_at[b, here, :]
-            projected_out[rows, cols] = flip(projected)
-            scale_out[rows, cols] = flip(projected / density)
-
-    for group_of in [[near], far, copies] + sent + pairs[0] + pairs[1] + pairs[2]:
-        for copy in group_of:
-            copy.wait_send()
+            projected_out[rows, cols] = flip(fitted_at[b, here, :])
+            density_in[rows, cols] = flip(change_at[b, here, :])
+            scale_out[rows, cols] = flip(1.0 / density)
+    drain(squares.at[pl.ds(0, slabs - 1)], sq_recv)
+    total = jnp.sum(jnp.sum(squares[...], axis=0), axis=(0, 1), keepdims=True)
+    mean_square = total * (1.0 / (height * width * slabs))
+    gain = step_cap / jnp.sqrt(mean_square + 1e-06)
+    for c in range(chunks):
+        rows = slice(c * TILE, (c + 1) * TILE)
+        projected = projected_out[rows, :] + gain * density_in[rows, :]
+        projected_out[rows, :] = projected
+        scale_out[rows, :] = projected * scale_out[rows, :]
+
+    drain(raws.at[pl.ds(0, 2)], halo_send)
+    drain(sent_bytes(2 * height), ens_send)
+    drain(partial, pair_send)
+    drain(squares.at[pl.ds(0, slabs - 1)], sq_send)
 
 
 def lift(finals, scale, projected, lifted_out, projected_out, scaled, sem):
-    copies = [pltpu.make_async_copy(projected, projected_out, sem.at[9])]
-    copies[0].start()
+    small = pltpu.make_async_copy(projected, projected_out, sem.at[1])
+    small.start()
     for i in range(9):
         scaled[i] = finals[i] * scale[...]
-        copy = pltpu.make_async_copy(scaled.at[i], lifted_out.at[0, i], sem.at[i])
-        copy.start()
-        copies.append(copy)
-    for copy in copies:
-        copy.wait()
+        pltpu.make_async_copy(scaled.at[i], lifted_out.at[0, i], sem.at[0]).start()
+    pltpu.make_async_copy(scaled, lifted_out.at[0], sem.at[0]).wait()
+    small.wait()
 
 
 def on_device(density0, relax_rate, perturbation):
@@ -506,18 +514,18 @@
             pltpu.VMEM((3, phases, blocks, TILE, LANES), f32),
             pltpu.VMEM((blocks, height, LANES), f32),
             pltpu.VMEM((blocks, height, LANES), f32),
-            pltpu.VMEM((slabs, TILE, LANES), f32),
+            pltpu.VMEM((slabs, 1, LANES), f32),
             dma((3,)),
             dma(()),
             dma(()),
             dma((chunks,)),
-            dma((chunks,)),
-            dma((PIECES, ens - 1)),
-            dma((PIECES, ens - 1)),
-            dma((3, phases, phases)),
-            dma((3, phases, phases)),
-            dma((slabs - 1,)),
-            dma((slabs - 1,)),
+            dma(()),
+            dma((2,)),
+            dma(()),
+            dma((phases,)),
+            dma(((phases - 1) * phases + 1,)),
+            dma(()),
+            dma(()),
         ],
         compiler_params=pltpu.CompilerParams(
             collective_id=0, has_side_effects=True, vmem_limit_bytes=48 << 20
@@ -528,7 +536,7 @@
         out_shape=(jax.ShapeDtypeStruct((1, 9, height, width), f32), field),
         in_specs=[vmem] * 3,
         out_specs=[hbm] * 2,
-        scratch_shapes=[pltpu.VMEM((9, height, width), f32), dma((10,))],
+        scratch_shapes=[pltpu.VMEM((9, height, width), f32), dma((2,))],
         compiler_params=pltpu.CompilerParams(vmem_limit_bytes=2 << 20),
     )(finals, scale, projected)
 

time: 29.2 us -> 28.5 us (0.976)
  Pallas kernels: 28.4 us -> 27.7 us
    pallas_call x1, Pallas kernels: 27.4 us -> 26.7 us  [on_device(): pl.pallas_call(functools.partial(kernel, ens, slabs), out_shape=(jax.Shap...]
where the time goes in v3:
time: 28.5 us; the launch traced here: 28.3 us
  Pallas kernels  27.7 us (97%)
  between operations  0.64 us (2%)
    pallas_call x1, Pallas kernels, on_device(): pl.pallas_call(functools.partial(kernel, ens, slabs), out_shape=(jax.Shap...  26.7 us
    pallas_call x1, Pallas kernels, on_device(): pl.pallas_call(lift, out_shape=(jax.ShapeDtypeStruct((1, 9, height, width...  0.95 us

profile of v3, /device:TPU:0, one launch (start us, length us, event | category | flops | bytes accessed | tf_op | source)
XLA Modules:
  0.0 28.3 jit_solution(12111806258295753427)
XLA Ops:
  0.6 26.7 %shard_map.50 = (f32[9,24,1024]{2,1,0:T(8,128)S(1)}, f32[24,1024]{1,0:T(8,128)S(1)}, f32[24,1024]{1,0:T(8,128)S(1)}) custom-call(f32[24,1024]{1,0:T(8,128)} %density_hbm.1, f32[24,1024]{1,0:T(8,128)} %relax_hbm.1, s32[1,24,1024]{2,1,0:T(8,128)} %pert_hbm.1), custom_call_target="tpu_custom_call" | custom-call | tf_op jit(solution)/shard_map/pallas_call | solution.py:496
  27.4 1.0 %shard_map.51 = (f32[1,9,24,1024]{3,2,1,0:T(8,128)}, f32[24,1024]{1,0:T(8,128)}) custom-call(f32[9,24,1024]{2,1,0:T(8,128)S(1)} %get-tuple-element.5.finals, f32[24,1024]{1,0:T(8,128)S(1)} %get-tuple-element.6.scale, f32[24,1024]{1,0:T(8,128)S(1)} %get-tuple-element.7.projected), custom_call_target="tpu_custom_call" | custom-call | tf_op jit(solution)/shard_map/pallas_call | solution.py:534

commit v4 on v3

--- a/solution.py
+++ b/solution.py
@@ -242,16 +242,6 @@
     for k in range(4, STEPS + 2):
         triangle(k)
 
-    near.wait_recv()
-    fill(NEAR, front + height, range(chunks))
-
-    def lean(t, base):
-        for n in range(4):
-            for j in range(chunks):
-                slot = jnp.where(t == 1, 0, DUMMY) if n == 3 else None
-                group(n % 2, base + (TILE * j - n), slot)
-        return base - 4
-
     def differing(mask):
         peer = me_e
         for n in range(phases):
@@ -270,6 +260,17 @@
                 device_id={"ens": differing(k)},
                 device_id_type=MESH,
             ).start()
+
+    send(0, STEPS, 2 * STEPS)
+    near.wait_recv()
+    fill(NEAR, front + height, range(chunks))
+
+    def lean(t, base):
+        for n in range(4):
+            for j in range(chunks):
+                slot = jnp.where(t == 1, 0, DUMMY) if n == 3 else None
+                group(n % 2, base + (TILE * j - n), slot)
+        return base - 4
 
     def sent_bytes(rows):
         return gathered.at[0, pl.ds(0, ens - 1), :, pl.ds(0, rows)]
@@ -323,13 +324,14 @@
     last = even if TOTAL % 2 == 0 else odd
     sample = {STEPS + 1: 0, 2 * STEPS + 1: 1}
     lax.fori_loop(0, 2, lean, height - 1)
-    send(0, STEPS, height)
-    for k in range(STEPS + 2, STEPS + 5):
+    send(0, 2 * STEPS, height)
+    ahead = 2 * STEPS + 2
+    for k in range(STEPS + 2, ahead):
         near_side(k)
+    send(1, 2 * STEPS, height)
     arrived(0)
     for n in range(TOTAL + 11):
         if n == 7:
-            send(1, 2 * STEPS, height)
             arrived(1)
         if n == 12:
             send(0, 0, STEPS)
@@ -344,8 +346,8 @@
                 copy.start()
         if n == 30:
             send_pairs(1, 1)
-        if STEPS + 5 + n <= TOTAL:
-            near_side(STEPS + 5 + n)
+        if ahead + n <= TOTAL:
+            near_side(ahead + n)
         strip(1, n + 2)
         strip(2, n - 5)
         strip(3, n - 10)

time: 28.5 us -> 28.6 us (level)
  no operation moved by 1% of the time
where the time goes in v4:
time: 28.6 us; the launch traced here: 28.4 us
  Pallas kernels  27.8 us (97%)
  between operations  0.64 us (2%)
    pallas_call x1, Pallas kernels, on_device(): pl.pallas_call(functools.partial(kernel, ens, slabs), out_shape=(jax.Shap...  26.8 us
    pallas_call x1, Pallas kernels, on_device(): pl.pallas_call(lift, out_shape=(jax.ShapeDtypeStruct((1, 9, height, width...  0.95 us

profile of v4, /device:TPU:0, one launch (start us, length us, event | category | flops | bytes accessed | tf_op | source)
XLA Modules:
  0.0 28.4 jit_solution(5958744766696068752)
XLA Ops:
  0.6 26.8 %shard_map.50 = (f32[9,24,1024]{2,1,0:T(8,128)S(1)}, f32[24,1024]{1,0:T(8,128)S(1)}, f32[24,1024]{1,0:T(8,128)S(1)}) custom-call(f32[24,1024]{1,0:T(8,128)} %density_hbm.1, f32[24,1024]{1,0:T(8,128)} %relax_hbm.1, s32[1,24,1024]{2,1,0:T(8,128)} %pert_hbm.1), custom_call_target="tpu_custom_call" | custom-call | tf_op jit(solution)/shard_map/pallas_call | solution.py:498
  27.4 1.0 %shard_map.51 = (f32[1,9,24,1024]{3,2,1,0:T(8,128)}, f32[24,1024]{1,0:T(8,128)}) custom-call(f32[9,24,1024]{2,1,0:T(8,128)S(1)} %get-tuple-element.5.finals, f32[24,1024]{1,0:T(8,128)S(1)} %get-tuple-element.6.scale, f32[24,1024]{1,0:T(8,128)S(1)} %get-tuple-element.7.projected), custom_call_target="tpu_custom_call" | custom-call | tf_op jit(solution)/shard_map/pallas_call | solution.py:536
